TPU v7x, 32 devices: a whole 2x2x4 slice. The times are simulated.
32 devices in a mesh: row: 4 (over x, core), col: 8 (over z, y).
Axes of the slice: x: 2, y: 2, z: 4, core: 2. Of those that a mesh axis runs over, the one named last changes fastest.
Arguments:
- factor: float32 [1, 8192, 512], P(None, ('row', 'col')), may hold values from -40 to 40, as said below
- update: float32 [1, 8192, 256], P(None, ('row', 'col')), may hold values from -1.5 to 1.5
Outputs:
- new_factor: float32 [1, 8192, 512], P(None, ('row', 'col'))
- new_update: float32 [1, 8192, 256], P(None, ('row', 'col'))
- column_scale: float32 [512], replicated
Inputs may be any that keep to these rules, and one draw needn't show every extreme that they name: `factor`: in the columns of panel p, rows of global tiles before p are zero; the diagonal block of panel p is lower triangular with diagonal entries of 1 to 2.
All inputs are finite; a program needn't handle non-finite values.
Results may differ from a plain program's by a relative error of at most 0.0003.
Values sent between devices are 32-bit elements; how exact they have to be, the bound alone decides.
No kernel may reach another device: no remote copies, remote signals or barrier semaphores. Data moves between devices by JAX's collectives and lax.ppermute only.
A program may use at most 64 MiB of HBM per device.

v0:
```python
import jax
import jax.numpy as jnp
from jax import lax
from jax.sharding import PartitionSpec as P

PW = 256
K = 256
PANELS = 2


def broadcast(array, axis, root):
    mine = lax.axis_index(axis) == root
    return lax.psum(jnp.where(mine, array, jnp.zeros_like(array)), axis)


def panel_terms(block_factor, block_update):
    highest = lax.Precision.HIGHEST
    gram_matrix = jnp.dot(block_factor, block_factor.T, precision=highest) + jnp.dot(
        block_update, block_update.T, precision=highest
    )
    diag_new = jnp.linalg.cholesky(gram_matrix)
    solved = lax.linalg.triangular_solve(block_factor, block_update, left_side=True, lower=True)
    inner_matrix = jnp.eye(K, dtype=jnp.float32) + jnp.dot(solved.T, solved, precision=highest)
    chol_inner = jnp.linalg.cholesky(inner_matrix)
    left_first = lax.linalg.triangular_solve(diag_new, block_factor, left_side=True, lower=True).T
    left_second = lax.linalg.triangular_solve(diag_new, block_update, left_side=True, lower=True).T
    right_first = lax.linalg.triangular_solve(
        chol_inner, jnp.eye(K, dtype=jnp.float32), left_side=True, lower=True
    ).T
    right_second = jnp.dot(solved, right_first, precision=highest)
    return (left_first, left_second, right_first, right_second)


def empty_terms(block_factor, block_update):
    return (
        jnp.zeros((PW, PW), jnp.float32),
        jnp.zeros((K, PW), jnp.float32),
        jnp.zeros((K, K), jnp.float32),
        jnp.zeros((PW, K), jnp.float32),
    )


def advance(panel_cols, current, transforms):
    highest = lax.Precision.HIGHEST
    left_first, left_second, right_first, right_second = transforms
    tile_count = panel_cols.shape[0]
    flat_cols = panel_cols.reshape(-1, PW)
    flat_update = current.reshape(-1, K)
    updated_cols = jnp.dot(flat_cols, left_first, precision=highest) + jnp.dot(
        flat_update, left_second, precision=highest
    )
    updated_rows = jnp.dot(flat_update, right_first, precision=highest) - jnp.dot(
        flat_cols, right_second, precision=highest
    )
    return (updated_cols.reshape(tile_count, PW, PW), updated_rows.reshape(tile_count, PW, K))


def on_device(factor, update):
    device_count = lax.axis_size(("row", "col"))
    my_index = lax.axis_index(("row", "col"))
    row_total = factor.shape[0] * device_count * PW
    current = update
    columns_out = []
    squares = []
    for panel_num in range(PANELS):
        low = panel_num * PW
        panel_cols = factor[:, :, low : low + PW]
        own_terms = lax.cond(
            my_index == panel_num, panel_terms, empty_terms, panel_cols[0], current[0]
        )
        transforms = jax.tree.map(
            lambda part: broadcast(part, ("row", "col"), panel_num), own_terms
        )
        updated_cols, current = advance(panel_cols, current, transforms)
        columns_out.append(updated_cols)
        local_squares = jnp.sum(updated_cols * updated_cols, axis=(0, 1))
        squares.append(lax.psum(local_squares, ("row", "col")))
    stacked = jnp.concatenate(squares, axis=0)
    column_scale = jnp.sqrt(stacked / row_total + 1e-06)
    return (jnp.concatenate(columns_out, axis=2), current, column_scale)


def solution(mesh):
    return jax.shard_map(
        on_device,
        mesh=mesh,
        in_specs=(P(None, ("row", "col"), None), P(None, ("row", "col"), None)),
        out_specs=(P(None, ("row", "col"), None), P(None, ("row", "col"), None), P()),
        check_vma=False,
    )
```

profile of v0, /device:TPU:0, one launch (start us, length us, event | category | flops | bytes accessed | tf_op | source)
XLA Modules:
  0.0 627.2 jit_solution(11467668654431806017)
XLA Ops:
  7.2 1.1 slice_bitcast_fusion.29
  8.3 150.0 %conditional.2 = (f32[256,256]{1,0:T(8,128)S(1)}, f32[256,256]{1,0:T(8,128)S(1)}, f32[256,256]{1,0:T(8,128)S(1)}, f32[256,256]{1,0:T(8,128)S(1)}) conditional(s32[]{:T(128)} %convert_element_type.18, () %tuple.26, (f32[256,256]{1,0:T(8,128)S(1)}, f32[256,256]{1,0:T(8,128)S(1)}) %tuple.188), branch_computations={%region_0.0_spmd, %region_1.8_spmd} | conditional | flops 1512079872 | bytes 17961552 | solution.py:68
  8.5 3.8 while.17
  8.5 0.6 fusion.130
  9.1 1.3 bitcast_dynamic-update-slice_fusion.16
  10.4 0.6 fusion.130
  11.0 1.3 bitcast_dynamic-update-slice_fusion.16
  12.3 19.8 %custom-call.24 = f32[2,128,128]{1,2,0:T(8,128)S(1)} custom-call(f32[2,128,128]{2,1,0:T(8,128)S(1)} %get-tuple-element.85), custom_call_target="InvertDiagBlocksLowerTriangular" | custom-call | tf_op jit(solution)/shard_map/cond/branch_1_fun/triangular_solve/custom-call.0 | solution.py:22
  32.1 0.3 fusion.10
  32.7 0.3 fusion.21
  33.0 0.6 convolution_add_fusion
  33.9 11.7 %cholesky.248 = f32[128,128]{1,0:T(8,128)S(1)} custom-call(f32[128,128]{1,0:T(8,128)S(1)} %cholesky.346), custom_call_target="Cholesky" | custom-call | tf_op jit(solution)/shard_map/cond/branch_1_fun/jit(cholesky)/cholesky | solution.py:24
  45.6 9.8 %custom-call.25 = f32[1,128,128]{1,2,0:T(8,128)S(1)} custom-call(f32[1,128,128]{2,1,0:T(8,128)S(1)} %get-tuple-element.181), custom_call_target="InvertDiagBlocksLowerTriangular" | custom-call | tf_op jit(solution)/shard_map/cond/branch_1_fun/jit(cholesky)/cholesky | solution.py:24
  55.7 0.3 convolution_subtract_fusion.4
  55.9 11.7 %cholesky.265 = f32[128,128]{1,0:T(8,128)S(1)} custom-call(f32[128,128]{1,0:T(8,128)S(1)} %convolution_subtract_fusion.4), custom_call_target="Cholesky" | custom-call | tf_op jit(solution)/shard_map/cond/branch_1_fun/jit(cholesky)/cholesky | solution.py:24
  67.7 0.6 compare_reduce_fusion
  69.6 3.8 while.18
  69.6 0.6 fusion.131
  70.2 1.3 bitcast_dynamic-update-slice_fusion.17
  71.6 0.6 fusion.131
  72.1 1.3 bitcast_dynamic-update-slice_fusion.17
  73.4 19.9 %custom-call.26 = f32[2,128,128]{1,2,0:T(8,128)S(1)} custom-call(f32[2,128,128]{2,1,0:T(8,128)S(1)} %get-tuple-element.86), custom_call_target="InvertDiagBlocksLowerTriangular" | custom-call | tf_op jit(solution)/shard_map/cond/branch_1_fun/triangular_solve/custom-call.0 | solution.py:27
  93.3 0.3 fusion.6
  93.7 0.4 convolution_subtract_fusion
  94.1 0.3 fusion.17
  94.4 0.4 fusion.4
  95.0 0.4 fusion.75
  95.4 0.4 convolution_add_fusion.1
  96.0 11.7 %cholesky.214 = f32[128,128]{1,0:T(8,128)S(1)} custom-call(f32[128,128]{1,0:T(8,128)S(1)} %cholesky.349), custom_call_target="Cholesky" | custom-call | tf_op jit(solution)/shard_map/cond/branch_1_fun/jit(cholesky)/cholesky | solution.py:21
  107.7 9.8 %custom-call.21 = f32[1,128,128]{1,2,0:T(8,128)S(1)} custom-call(f32[1,128,128]{2,1,0:T(8,128)S(1)} %get-tuple-element.177), custom_call_target="InvertDiagBlocksLowerTriangular" | custom-call | tf_op jit(solution)/shard_map/cond/branch_1_fun/jit(cholesky)/cholesky | solution.py:21
  118.1 11.9 %cholesky.231 = f32[128,128]{1,0:T(8,128)S(1)} custom-call(f32[128,128]{1,0:T(8,128)S(1)} %convolution_subtract_fusion.5), custom_call_target="Cholesky" | custom-call | tf_op jit(solution)/shard_map/cond/branch_1_fun/jit(cholesky)/cholesky | solution.py:21
  130.0 0.6 compare_reduce_fusion.2
  132.0 4.0 while.16
  132.1 0.6 fusion.129
  132.6 1.4 bitcast_dynamic-update-slice_fusion.15
  134.1 0.6 fusion.129
  134.6 1.4 bitcast_dynamic-update-slice_fusion.15
  136.0 19.7 %custom-call.22 = f32[2,128,128]{1,2,0:T(8,128)S(1)} custom-call(f32[2,128,128]{2,1,0:T(8,128)S(1)} %get-tuple-element.83), custom_call_target="InvertDiagBlocksLowerTriangular" | custom-call | tf_op jit(solution)/shard_map/cond/branch_1_fun/triangular_solve/custom-call.0 | solution.py:25
  155.7 0.3 fusion.12
  156.0 0.3 fusion.8
  156.9 0.3 fusion.24
  157.2 0.3 fusion.25
  158.3 0.7 broadcast_select_fusion.5
  159.1 0.7 broadcast_select_fusion.4
  159.9 0.8 broadcast_select_fusion.6
  160.7 124.5 %all-reduce.9.cloned.1.call-done = (f32[256,256]{1,0:T(8,128)}, f32[256,256]{1,0:T(8,128)}) async-done(((f32[256,256]{1,0:T(8,128)}, f32[256,256]{1,0:T(8,128)}), (f32[256,256]{1,0:T(8,128)}, f32[256,256]{1,0:T(8,128)})) %all-reduce.9.cloned.1.call-update) | async-done | bytes 524304 | tf_op jit(solution)/shard_map/psum | solution.py:13
  285.1 1.6 fusion.65
  286.7 0.6 convolution_subtract_fusion.12
  287.4 4.7 conditional.3
  287.5 0.7 broadcast.78.clone
  292.0 0.8 broadcast_select_fusion.2
  292.9 0.8 broadcast_select_fusion
  293.7 279.4 %all-reduce.7.cloned.1.call-done = (f32[256,256]{1,0:T(8,128)}, f32[256,256]{1,0:T(8,128)}, f32[256,256]{1,0:T(8,128)}, f32[256,256]{1,0:T(8,128)}, f32[256,256]{1,0:T(8,128)}, /*index=5*/f32[256,256]{1,0:T(8,128)}) async-done(((f32[256,256]{1,0:T(8,128)}, f32[256,256]{1,0:T(8,128)}, f32[256,256]{1,0:T(8,128)}, f32[256,256]{1,0:T(8,128)}, f32[256,256]{1,0:T(8,128)}, /*index=5*/f32[256,256]{1,0:T(8,128)}), ...) | async-done | bytes 1572880 | tf_op jit(solution)/shard_map/psum | solution.py:13
  573.2 1.6 convolution_bitcast_fusion.1
  574.8 0.6 fusion.77
  575.4 0.3 copy-done.4
  575.7 0.6 fusion.68
  576.3 0.3 copy-done.3
  576.7 0.7 multiply_reduce_fusion
  577.6 0.7 fusion.62
  578.4 1.0 copy.26
  579.4 1.1 fusion.61
  580.5 39.0 %all-reduce.1 = (f32[256]{0:T(256)S(1)}, f32[256]{0:T(256)S(1)}) all-reduce(f32[256]{0:T(256)S(1)} %get-tuple-element.214, f32[256]{0:T(256)S(1)} %get-tuple-element.216), channel_id=1, replica_groups=mesh['row'=4,'col'=8] {'row','col'}, use_global_device_ids=true, to_apply=%region_19.22 | all-reduce | flops 512 | bytes 4096 | tf_op jit(solution)/shard_map/psum | solution.py:77
  619.5 0.6 fusion.64
  (61 shorter events, 3.2 us)
Async XLA Ops:
  7.2 278.0 %all-reduce.9.cloned.1.call-start = ((), (), s32[]{:S(2)}) async-start(), calls=%async_computation.1 | async-start | bytes 1048576 | tf_op jit(solution)/shard_map/psum | solution.py:13
  7.2 1.1 copy-start
  159.8 413.4 %all-reduce.7.cloned.1.call-start = ((), (), s32[]{:S(2)}) async-start(), calls=%async_computation | async-start | bytes 3145728 | tf_op jit(solution)/shard_map/psum | solution.py:13
  160.7 126.0 %copy-start.1 = (f32[1,256,512]{2,1,0:T(8,128)S(1)}, f32[1,256,512]{2,1,0:T(8,128)}, u32[]{:S(2)}) copy-start(f32[1,256,512]{2,1,0:T(8,128)} %param.9) | copy-start | bytes 1572868
  285.1 1.6 copy-start.7
  573.2 1.6 copy-start.5
  574.8 1.0 copy-start.4
  575.7 0.9 copy-start.3
  576.7 0.9 copy-start.2
  578.4 1.0 copy-start.6
Sparse Core Ops, SparseCore 0:
  159.9 125.1 all-reduce.8
  293.9 279.2 all-reduce.6
where the time goes:
time: 630 us; the launch traced here: 627 us
  waiting for transfers between devices  404 us (64%)
  other arithmetic  132 us (21%)
  blocking collectives  39 us (6%)
  local copies, waits for them, and re-layouts  16.1 us (3%)
  between operations  14.4 us (2%)
  matrix products  13.8 us (2%)
  loops' own time  7.43 us (1%)
    psum x2, waiting for transfers between devices, broadcast(): return lax.psum(jnp.where(mine, array, jnp.zeros_like(array)), axis)  404 us
    psum x1, blocking collectives, on_device(): squares.append(lax.psum(local_squares, ('row', 'col')))  39 us
    another operation x6, other arithmetic, panel_terms(): diag_new = jnp.linalg.cholesky(gram_matrix)  34.2 us
    another operation x6, other arithmetic, panel_terms(): chol_inner = jnp.linalg.cholesky(inner_matrix)  33.9 us
    another operation x2, other arithmetic, panel_terms(): lax.linalg.triangular_solve(chol_inner, jnp.eye(K, dtype=jnp.float32), le...  19.9 us
    another operation x2, other arithmetic, panel_terms(): lax.linalg.triangular_solve(block_factor, block_update, left_side=True, l...  19.9 us
    another operation x3, other arithmetic, panel_terms(): lax.linalg.triangular_solve(diag_new, block_factor, left_side=True, lower...  19.7 us
  transfers between devices with their start and end apart: 2, of which 2 were waited for; matrix products, arithmetic and copies ran while one was open for 0% of the time, Pallas kernels for 0%

commit v1 on v0

--- a/solution.py
+++ b/solution.py
@@ -74,7 +74,7 @@
         updated_cols, current = advance(panel_cols, current, transforms)
         columns_out.append(updated_cols)
         local_squares = jnp.sum(updated_cols * updated_cols, axis=(0, 1))
-        squares.append(lax.psum(local_squares, ("row", "col")))
+        squares.append(jnp.sum(lax.all_gather(local_squares, ("row", "col")), axis=0))
     stacked = jnp.concatenate(squares, axis=0)
     column_scale = jnp.sqrt(stacked / row_total + 1e-06)
     return (jnp.concatenate(columns_out, axis=2), current, column_scale)

time: 630 us -> 720 us (1.14)
  blocking collectives: 39 us -> 129 us
    all_gather x0 -> x2, blocking collectives: none -> 129 us  [on_device(): lax.all_gather(local_squares, ('row', 'col'))]
    psum x1 -> x0, blocking collectives: 39 us -> none  [on_device(): squares.append(lax.psum(local_squares, ('row', 'col')))]
where the time goes in v1:
time: 720 us; the launch traced here: 717 us
  waiting for transfers between devices  404 us (56%)
  other arithmetic  132 us (18%)
  blocking collectives  129 us (18%)
  local copies, waits for them, and re-layouts  16.1 us (2%)
  between operations  14.4 us (2%)
  matrix products  13.8 us (2%)
  loops' own time  7.22 us (1%)
    psum x2, waiting for transfers between devices, broadcast(): return lax.psum(jnp.where(mine, array, jnp.zeros_like(array)), axis)  404 us
    all_gather x2, blocking collectives, on_device(): lax.all_gather(local_squares, ('row', 'col'))  129 us
    another operation x6, other arithmetic, panel_terms(): diag_new = jnp.linalg.cholesky(gram_matrix)  34.2 us
    another operation x6, other arithmetic, panel_terms(): chol_inner = jnp.linalg.cholesky(inner_matrix)  33.9 us
    another operation x2, other arithmetic, panel_terms(): lax.linalg.triangular_solve(chol_inner, jnp.eye(K, dtype=jnp.float32), le...  19.9 us
    another operation x2, other arithmetic, panel_terms(): lax.linalg.triangular_solve(block_factor, block_update, left_side=True, l...  19.9 us
    another operation x3, other arithmetic, panel_terms(): lax.linalg.triangular_solve(diag_new, block_factor, left_side=True, lower...  19.7 us
  transfers between devices with their start and end apart: 2, of which 2 were waited for; matrix products, arithmetic and copies ran while one was open for 0% of the time, Pallas kernels for 0%

profile of v1, /device:TPU:0, one launch (start us, length us, event | category | flops | bytes accessed | tf_op | source)
XLA Modules:
  0.0 717.4 jit_solution(5631657694311954855)
XLA Ops:
  7.2 1.1 slice_bitcast_fusion.29
  8.3 150.0 %conditional.2 = (f32[256,256]{1,0:T(8,128)S(1)}, f32[256,256]{1,0:T(8,128)S(1)}, f32[256,256]{1,0:T(8,128)S(1)}, f32[256,256]{1,0:T(8,128)S(1)}) conditional(s32[]{:T(128)} %convert_element_type.18, () %tuple.26, (f32[256,256]{1,0:T(8,128)S(1)}, f32[256,256]{1,0:T(8,128)S(1)}) %tuple.192), branch_computations={%region_0.0_spmd, %region_1.8_spmd} | conditional | flops 1512079872 | bytes 17961552 | solution.py:68
  8.5 3.8 while.17
  8.5 0.6 fusion.130
  9.1 1.3 bitcast_dynamic-update-slice_fusion.16
  10.4 0.6 fusion.130
  11.0 1.3 bitcast_dynamic-update-slice_fusion.16
  12.3 19.8 %custom-call.24 = f32[2,128,128]{1,2,0:T(8,128)S(1)} custom-call(f32[2,128,128]{2,1,0:T(8,128)S(1)} %get-tuple-element.85), custom_call_target="InvertDiagBlocksLowerTriangular" | custom-call | tf_op jit(solution)/shard_map/cond/branch_1_fun/triangular_solve/custom-call.0 | solution.py:22
  32.1 0.3 fusion.10
  32.7 0.3 fusion.21
  33.0 0.6 convolution_add_fusion
  33.9 11.7 %cholesky.248 = f32[128,128]{1,0:T(8,128)S(1)} custom-call(f32[128,128]{1,0:T(8,128)S(1)} %cholesky.346), custom_call_target="Cholesky" | custom-call | tf_op jit(solution)/shard_map/cond/branch_1_fun/jit(cholesky)/cholesky | solution.py:24
  45.6 9.8 %custom-call.25 = f32[1,128,128]{1,2,0:T(8,128)S(1)} custom-call(f32[1,128,128]{2,1,0:T(8,128)S(1)} %get-tuple-element.192), custom_call_target="InvertDiagBlocksLowerTriangular" | custom-call | tf_op jit(solution)/shard_map/cond/branch_1_fun/jit(cholesky)/cholesky | solution.py:24
  55.9 11.7 %cholesky.265 = f32[128,128]{1,0:T(8,128)S(1)} custom-call(f32[128,128]{1,0:T(8,128)S(1)} %convolution_subtract_fusion.4), custom_call_target="Cholesky" | custom-call | tf_op jit(solution)/shard_map/cond/branch_1_fun/jit(cholesky)/cholesky | solution.py:24
  67.7 0.6 compare_reduce_fusion
  69.6 3.8 while.18
  69.6 0.6 fusion.131
  70.2 1.3 bitcast_dynamic-update-slice_fusion.17
  71.6 0.6 fusion.131
  72.1 1.3 bitcast_dynamic-update-slice_fusion.17
  73.4 19.9 %custom-call.26 = f32[2,128,128]{1,2,0:T(8,128)S(1)} custom-call(f32[2,128,128]{2,1,0:T(8,128)S(1)} %get-tuple-element.86), custom_call_target="InvertDiagBlocksLowerTriangular" | custom-call | tf_op jit(solution)/shard_map/cond/branch_1_fun/triangular_solve/custom-call.0 | solution.py:27
  93.3 0.3 fusion.6
  93.7 0.4 convolution_subtract_fusion
  94.1 0.3 fusion.17
  94.4 0.4 fusion.4
  95.0 0.4 fusion.75
  95.4 0.4 convolution_add_fusion.1
  96.0 11.7 %cholesky.214 = f32[128,128]{1,0:T(8,128)S(1)} custom-call(f32[128,128]{1,0:T(8,128)S(1)} %cholesky.349), custom_call_target="Cholesky" | custom-call | tf_op jit(solution)/shard_map/cond/branch_1_fun/jit(cholesky)/cholesky | solution.py:21
  107.7 9.8 %custom-call.21 = f32[1,128,128]{1,2,0:T(8,128)S(1)} custom-call(f32[1,128,128]{2,1,0:T(8,128)S(1)} %get-tuple-element.188), custom_call_target="InvertDiagBlocksLowerTriangular" | custom-call | tf_op jit(solution)/shard_map/cond/branch_1_fun/jit(cholesky)/cholesky | solution.py:21
  118.1 11.9 %cholesky.231 = f32[128,128]{1,0:T(8,128)S(1)} custom-call(f32[128,128]{1,0:T(8,128)S(1)} %convolution_subtract_fusion.5), custom_call_target="Cholesky" | custom-call | tf_op jit(solution)/shard_map/cond/branch_1_fun/jit(cholesky)/cholesky | solution.py:21
  130.0 0.6 compare_reduce_fusion.2
  132.0 4.0 while.16
  132.1 0.6 fusion.129
  132.6 1.4 bitcast_dynamic-update-slice_fusion.15
  134.1 0.6 fusion.129
  134.6 1.4 bitcast_dynamic-update-slice_fusion.15
  136.0 19.7 %custom-call.22 = f32[2,128,128]{1,2,0:T(8,128)S(1)} custom-call(f32[2,128,128]{2,1,0:T(8,128)S(1)} %get-tuple-element.83), custom_call_target="InvertDiagBlocksLowerTriangular" | custom-call | tf_op jit(solution)/shard_map/cond/branch_1_fun/triangular_solve/custom-call.0 | solution.py:25
  155.7 0.3 fusion.12
  156.0 0.3 fusion.8
  156.9 0.3 fusion.24
  157.2 0.3 fusion.25
  158.3 0.7 broadcast_select_fusion.5
  159.1 0.7 broadcast_select_fusion.4
  159.9 0.8 broadcast_select_fusion.6
  160.7 124.5 %all-reduce.8.cloned.1.call-done = (f32[256,256]{1,0:T(8,128)}, f32[256,256]{1,0:T(8,128)}) async-done(((f32[256,256]{1,0:T(8,128)}, f32[256,256]{1,0:T(8,128)}), (f32[256,256]{1,0:T(8,128)}, f32[256,256]{1,0:T(8,128)})) %all-reduce.8.cloned.1.call-update) | async-done | bytes 524304 | tf_op jit(solution)/shard_map/psum | solution.py:13
  285.1 1.6 fusion.65
  286.7 0.6 convolution_subtract_fusion.12
  287.4 4.5 conditional.3
  287.5 0.7 broadcast.78.clone
  291.8 0.8 broadcast_select_fusion.2
  292.7 0.8 broadcast_select_fusion
  293.5 279.7 %all-reduce.6.cloned.1.call-done = (f32[256,256]{1,0:T(8,128)}, f32[256,256]{1,0:T(8,128)}, f32[256,256]{1,0:T(8,128)}, f32[256,256]{1,0:T(8,128)}, f32[256,256]{1,0:T(8,128)}, /*index=5*/f32[256,256]{1,0:T(8,128)}) async-done(((f32[256,256]{1,0:T(8,128)}, f32[256,256]{1,0:T(8,128)}, f32[256,256]{1,0:T(8,128)}, f32[256,256]{1,0:T(8,128)}, f32[256,256]{1,0:T(8,128)}, /*index=5*/f32[256,256]{1,0:T(8,128)}), ...) | async-done | bytes 1572880 | tf_op jit(solution)/shard_map/psum | solution.py:13
  573.2 1.6 convolution_bitcast_fusion.1
  574.8 0.6 fusion.77
  575.4 0.3 copy-done.4
  575.8 0.6 fusion.68
  576.4 0.3 copy-done.3
  576.7 0.7 multiply_reduce_fusion
  577.6 0.7 fusion.62
  578.4 1.0 copy.48
  579.4 65.0 %all-gather.3 = f32[32,1,256]{2,1,0:T(1,128)S(1)} all-gather(f32[1,1,256]{2,1,0:T(1,128)S(1)} %bitcast.247), channel_id=3, replica_groups=mesh['row'=4,'col'=8] {'row','col'}, dimensions={0}, use_global_device_ids=true | all-gather | bytes 33792 | tf_op jit(solution)/shard_map/all_gather | solution.py:77
  644.4 64.2 %all-gather.2 = f32[32,1,256]{2,1,0:T(1,128)S(1)} all-gather(f32[1,1,256]{2,1,0:T(1,128)S(1)} %bitcast.248), channel_id=2, replica_groups=mesh['row'=4,'col'=8] {'row','col'}, dimensions={0}, use_global_device_ids=true | all-gather | bytes 33792 | tf_op jit(solution)/shard_map/all_gather | solution.py:77
  708.7 1.1 fusion.61
  709.8 0.6 fusion.64
  (64 shorter events, 3.6 us)
Async XLA Ops:
  7.2 278.0 %all-reduce.8.cloned.1.call-start = ((), (), s32[]{:S(2)}) async-start(), calls=%async_computation.1 | async-start | bytes 1048576 | tf_op jit(solution)/shard_map/psum | solution.py:13
  7.2 1.1 copy-start
  159.8 413.4 %all-reduce.6.cloned.1.call-start = ((), (), s32[]{:S(2)}) async-start(), calls=%async_computation | async-start | bytes 3145728 | tf_op jit(solution)/shard_map/psum | solution.py:13
  160.7 126.0 %copy-start.1 = (f32[1,256,512]{2,1,0:T(8,128)S(1)}, f32[1,256,512]{2,1,0:T(8,128)}, u32[]{:S(2)}) copy-start(f32[1,256,512]{2,1,0:T(8,128)} %param.9) | copy-start | bytes 1572868
  285.1 1.6 copy-start.7
  573.2 1.6 copy-start.5
  574.8 1.0 copy-start.4
  575.7 0.9 copy-start.3
  576.7 0.9 copy-start.2
  578.4 130.3 %copy-start.6 = (f32[256,256]{1,0:T(8,128)S(1)}, f32[256,256]{1,0:T(8,128)}, u32[]{:S(2)}) copy-start(f32[256,256]{1,0:T(8,128)} %get-tuple-element.176) | copy-start | bytes 786436
Sparse Core Ops, SparseCore 0:
  159.9 125.1 all-reduce.7
  293.7 279.4 all-reduce.5
